TPU v7x, 128 devices: a whole 4x4x4 slice. The times are simulated.
128 devices in a mesh: dp: 16 (over y, x), row: 2 (over core), col: 4 (over z).
Axes of the slice: x: 4, y: 4, z: 4, core: 2. Of those that a mesh axis runs over, the one named last changes fastest.
Arguments:
- tokens: bfloat16 [15360, 4096], P(('dp', 'col'), 'row'), may hold values from -6 to 6
- hidden_cot: bfloat16 [15360, 14336], P(('dp', 'row'), 'col'), may hold values from -0.048339844 to 0.048339844
- gate_pre: bfloat16 [15360, 14336], P(('dp', 'row'), 'col'), may hold values from -10 to 10
- up_pre: bfloat16 [15360, 14336], P(('dp', 'row'), 'col'), may hold values from -6 to 6
Outputs:
- grad_gate: bfloat16 [2, 2048, 14336], P('row', 'dp', 'col')
All inputs are finite; a program needn't handle non-finite values.
Results may differ from a plain program's by a relative error of at most 0.014.
Values may be sent and summed in bfloat16 or wider, within the bound.
A program may use at most 128 MiB of HBM per device.

v0:
```python
import jax
import jax.numpy as jnp
from jax import lax
from jax.sharding import PartitionSpec as P


def copy_for_each(x, axis):
    copies = jnp.broadcast_to(x, (lax.axis_size(axis), *x.shape))
    return lax.all_to_all(copies, axis, split_axis=0, concat_axis=0, tiled=True)


def in_order(tiles, dim):
    lengths = list(tiles.shape[1:])
    lengths[dim] *= tiles.shape[0]
    return jnp.moveaxis(tiles, 0, dim).reshape(lengths)


def gather_directly(x, axis, dim):
    tiles = copy_for_each(x, axis)
    return in_order(tiles, dim)


def contract_rows(left, right):
    return lax.dot_general(
        left, right, (((0,), (0,)), ((), ())), preferred_element_type=jnp.float32
    )


def on_device(tokens, hidden_cot, gate_pre, up_pre):
    tok_full = lax.all_gather(tokens, "col", axis=0, tiled=True)
    gate_val = gate_pre.astype(jnp.float32)
    up_val = up_pre.astype(jnp.float32)
    cot_val = hidden_cot.astype(jnp.float32)
    sigma = jax.nn.sigmoid(gate_val)
    gate_grad = (cot_val * up_val * sigma * (1.0 + gate_val * (1.0 - sigma))).astype(jnp.bfloat16)
    group_part = contract_rows(tok_full, gather_directly(gate_grad, "row", 0))
    summed = lax.psum_scatter(
        group_part.astype(jnp.bfloat16), "dp", scatter_dimension=0, tiled=True
    )
    return summed.reshape(1, summed.shape[0], summed.shape[1])


def solution(mesh):
    in_specs = (
        P(("dp", "col"), "row"),
        P(("dp", "row"), "col"),
        P(("dp", "row"), "col"),
        P(("dp", "row"), "col"),
    )
    out_specs = P("row", "dp", "col")
    return jax.shard_map(
        on_device, mesh=mesh, in_specs=in_specs, out_specs=out_specs, check_vma=False
    )
```

profile of v0, /device:TPU:1, one launch (start us, length us, event | category | flops | bytes accessed | tf_op | source)
XLA Modules:
  0.0 211.0 jit_solution(15205189420382269202)
XLA Ops:
  6.5 0.0 all-gather.2.cloned.1.call-start
  6.5 0.7 all-gather.2.cloned.1.call-update
  7.3 0.0 reduce-scatter.4.cloned.1.call-start
  7.3 5.6 %fusion.6 = bf16[480,3584]{1,0:T(8,128)(2,1)S(1)} fusion(bf16[480,3584]{1,0:T(8,128)(2,1)} %param.6, bf16[480,3584]{1,0:T(8,128)(2,1)} %param.7, bf16[480,3584]{1,0:T(8,128)(2,1)} %param.5), kind=kLoop, calls=%fused_computation.9 | loop fusion | flops 22364160 | bytes 13762560 | tf_op jit(solution)/shard_map/convert_element_type | solution.py:35
  12.9 0.4 broadcast_in_dim.3
  13.3 11.5 %all_to_all.5 = bf16[2,480,3584]{2,1,0:T(8,128)(2,1)} all-to-all(bf16[2,480,3584]{2,1,0:T(8,128)(2,1)S(1)} %broadcast_in_dim.3), channel_id=1, replica_groups=mesh['dp'=16,'row'=2,'col'=4] {'row'}, dimensions={0} | all-to-all | bytes 13762560 | tf_op jit(solution)/shard_map/all_to_all | solution.py:9
  24.8 33.5 %all-gather.2.cloned.1.call-done = bf16[960,2048]{1,0:T(8,128)(2,1)} async-done(((bf16[240,2048]{1,0:T(8,128)(2,1)}), bf16[960,2048]{1,0:T(8,128)(2,1)}) %all-gather.2.cloned.1.call-update) | async-done | bytes 3932176 | tf_op jit(solution)/shard_map/all_gather | solution.py:30
  58.3 21.9 %fusion = bf16[2048,3584]{0,1:T(8,128)(2,1)} fusion(bf16[960,3584]{1,0:T(8,128)(2,1)} %bitcast.7, bf16[960,2048]{1,0:T(8,128)(2,1)} %all-gather.2.cloned.1.call-done), kind=kOutput, calls=%fused_computation.1 | convolution fusion | flops 14100201472 | bytes 25493504 | tf_op jit(solution)/shard_map/dot_general | solution.py:24
  80.2 18.6 %copy.7 = bf16[2048,3584]{1,0:T(8,128)(2,1)} copy(bf16[2048,3584]{0,1:T(8,128)(2,1)} %fusion) | data formatting | bytes 29360128
  98.8 0.0 reduce-scatter.4.cloned.1.call-update
  98.9 102.5 %reduce-scatter.4.cloned.1.call-done = bf16[128,3584]{1,0:T(8,128)(2,1)} async-done(((bf16[2048,3584]{1,0:T(8,128)(2,1)}), bf16[128,3584]{1,0:T(8,128)(2,1)}) %reduce-scatter.4.cloned.1.call-update) | async-done | bytes 917520
  201.4 1.5 copy.8
  202.9 1.3 copy.6
Async XLA Ops:
  6.5 51.8 %all-gather.2.cloned.1.call-start = ((), (), s32[]{:S(2)}) async-start(), calls=%async_computation.2 | async-start | bytes 4915200 | tf_op jit(solution)/shard_map/all_gather | solution.py:30
  7.3 194.1 %reduce-scatter.4.cloned.1.call-start = ((), (), s32[]{:S(2)}) async-start(), calls=%async_computation.3 | async-start | bytes 15597568
Sparse Core Ops, SparseCore 0:
  9.0 49.2 all-gather.1
  99.0 102.3 reduce-scatter.3
where the time goes:
time: 212 us; the launch traced here: 211 us
  waiting for transfers between devices  137 us (65%)
  local copies, waits for them, and re-layouts  21.9 us (10%)
  matrix products  21.9 us (10%)
  between operations  13.4 us (6%)
  blocking collectives  11.5 us (5%)
  other arithmetic  5.55 us (3%)
    unnamed x3, waiting for transfers between devices  103 us
    all_gather x1, waiting for transfers between devices, on_device(): tok_full = lax.all_gather(tokens, 'col', axis=0, tiled=True)  33.5 us
    dot_general x1, matrix products, contract_rows(): lax.dot_general(left, right, (((0,), (0,)), ((), ())), preferred_element_...  21.9 us
    unnamed x2, local copies, waits for them, and re-layouts  20.2 us
    all_to_all x1, blocking collectives, copy_for_each(): return lax.all_to_all(copies, axis, split_axis=0, concat_axis=0, tiled=True)  11.5 us
    convert_element_type x1, other arithmetic, on_device(): (cot_val * up_val * sigma * (1.0 + gate_val * (1.0 - sigma))).astype(jnp....  5.55 us
  transfers between devices with their start and end apart: 2, of which 2 were waited for; matrix products, arithmetic and copies ran while one was open for 3% of the time, Pallas kernels for 0%

commit v1 on v0

--- a/solution.py
+++ b/solution.py
@@ -2,6 +2,11 @@
 import jax.numpy as jnp
 from jax import lax
 from jax.sharding import PartitionSpec as P
+
+
+def gather_by_exchange(shard, axis, dim):
+    copies = jnp.concatenate([shard] * lax.axis_size(axis), axis=dim)
+    return lax.all_to_all(copies, axis, dim, dim, tiled=True)
 
 
 def copy_for_each(x, axis):
@@ -27,7 +32,7 @@
 
 
 def on_device(tokens, hidden_cot, gate_pre, up_pre):
-    tok_full = lax.all_gather(tokens, "col", axis=0, tiled=True)
+    tok_full = gather_by_exchange(tokens, "col", 0)
     gate_val = gate_pre.astype(jnp.float32)
     up_val = up_pre.astype(jnp.float32)
     cot_val = hidden_cot.astype(jnp.float32)

time: 212 us -> 211 us (level)
  blocking collectives: 11.5 us -> 50.3 us
  waiting for transfers between devices: 137 us -> 107 us
  local copies, waits for them, and re-layouts: 21.9 us -> 3.26 us
  starting transfers between devices: 0.04 us -> 7.95 us
  other arithmetic: 5.55 us -> 7.77 us
    unnamed x3 -> x1, waiting for transfers between devices: 103 us -> 0.02 us
    reduce_scatter x0 -> x1, waiting for transfers between devices: none -> 103 us  [on_device(): lax.psum_scatter(group_part.astype(jnp.bfloat16), 'dp', scatter_dimension...]
    all_to_all x1, blocking collectives: 11.5 us -> 50.3 us  [gather_by_exchange(): return lax.all_to_all(copies, axis, dim, dim, tiled=True)]
    all_gather x1 -> x0, waiting for transfers between devices: 33.5 us -> none  [on_device(): tok_full = lax.all_gather(tokens, 'col', axis=0, tiled=True)]
    unnamed x2, local copies, waits for them, and re-layouts: 20.2 us -> 0.01 us
    all_to_all x0 -> x1, starting transfers between devices: none -> 7.95 us  [copy_for_each(): return lax.all_to_all(copies, axis, split_axis=0, concat_axis=0, tiled=True)]
    all_to_all x0 -> x1, waiting for transfers between devices: none -> 3.82 us  [copy_for_each(): return lax.all_to_all(copies, axis, split_axis=0, concat_axis=0, tiled=True)]
    broadcast_in_dim x1, local copies, waits for them, and re-layouts: 0.44 us -> 3.26 us  [copy_for_each(): copies = jnp.broadcast_to(x, (lax.axis_size(axis), *x.shape))]
  transfers between devices with their start and end apart: 2 -> 2, of which waited for: 2 -> 2; matrix products, arithmetic and copies ran while one was open for 3% -> 1% of each run, Pallas kernels for 0% -> 0%
where the time goes in v1:
time: 211 us
  waiting for transfers between devices  107 us (51%)
  blocking collectives  50.3 us (24%)
  matrix products  20.9 us (10%)
  between operations  13.4 us (6%)
  starting transfers between devices  7.95 us (4%)
  other arithmetic  7.77 us (4%)
  local copies, waits for them, and re-layouts  3.26 us (2%)
    reduce_scatter x1, waiting for transfers between devices, on_device(): lax.psum_scatter(group_part.astype(jnp.bfloat16), 'dp', scatter_dimension...  103 us
    all_to_all x1, blocking collectives, gather_by_exchange(): return lax.all_to_all(copies, axis, dim, dim, tiled=True)  50.3 us
    dot_general x1, matrix products, contract_rows(): lax.dot_general(left, right, (((0,), (0,)), ((), ())), preferred_element_...  20.9 us
    all_to_all x1, starting transfers between devices, copy_for_each(): return lax.all_to_all(copies, axis, split_axis=0, concat_axis=0, tiled=True)  7.95 us
    convert_element_type x1, other arithmetic, on_device(): (cot_val * up_val * sigma * (1.0 + gate_val * (1.0 - sigma))).astype(jnp....  5.55 us
  transfers between devices with their start and end apart: 2, of which 2 were waited for; matrix products, arithmetic and copies ran while one was open for 1% of the time, Pallas kernels for 0%

profile of v1, /device:TPU:1, one launch (start us, length us, event | category | flops | bytes accessed | tf_op | source)
XLA Modules:
  0.0 210.5 jit_solution(18097276510412270551)
XLA Ops:
  6.5 5.5 %fusion.5 = bf16[480,3584]{1,0:T(8,128)(2,1)S(1)} fusion(bf16[480,3584]{1,0:T(8,128)(2,1)} %param.6, bf16[480,3584]{1,0:T(8,128)(2,1)} %param.7, bf16[480,3584]{1,0:T(8,128)(2,1)} %param.5), kind=kLoop, calls=%fused_computation.8 | loop fusion | flops 22364160 | bytes 13762560 | tf_op jit(solution)/shard_map/convert_element_type | solution.py:40
  12.1 3.3 %broadcast_in_dim.3 = bf16[2,480,3584]{2,1,0:T(8,128)(2,1)} broadcast(bf16[480,3584]{1,0:T(8,128)(2,1)S(1)} %fusion.5), dimensions={1,2} | broadcast | bytes 10321920 | tf_op jit(solution)/shard_map/broadcast_in_dim | solution.py:13
  15.3 0.0 copy-start
  15.4 8.0 %all-to-all-start.1 = ((bf16[2,480,3584]{2,1,0:T(8,128)(2,1)}), bf16[2,480,3584]{2,1,0:T(8,128)(2,1)}, u32[]{:S(2)}, u32[]{:S(2)}) async-start(bf16[2,480,3584]{2,1,0:T(8,128)(2,1)} %broadcast_in_dim.3), calls=%async_computation.1 | async-start | bytes 13762560 | tf_op jit(solution)/shard_map/all_to_all | solution.py:14
  23.3 0.0 reduce-scatter.2.cloned.1.call-start
  23.3 0.0 copy-done
  23.3 2.2 %pad_maximum_fusion = bf16[960,2048]{1,0:T(8,128)(2,1)} fusion(bf16[240,2048]{1,0:T(8,128)(2,1)S(1)} %copy-done), kind=kLoop, calls=%fused_computation.9 | loop fusion | flops 15728640 | bytes 4915200 | tf_op jit(solution)/shard_map/concatenate | solution.py:8
  25.5 3.8 %all-to-all-done.1 = bf16[2,480,3584]{2,1,0:T(8,128)(2,1)} async-done(((bf16[2,480,3584]{2,1,0:T(8,128)(2,1)}), bf16[2,480,3584]{2,1,0:T(8,128)(2,1)}, u32[]{:S(2)}, u32[]{:S(2)}) %all-to-all-start.1) | async-done | bytes 6881312 | tf_op jit(solution)/shard_map/all_to_all | solution.py:14
  29.4 50.3 %all_to_all.17 = bf16[4,240,2048]{2,1,0:T(8,128)(2,1)S(1)} all-to-all(bf16[4,240,2048]{2,1,0:T(8,128)(2,1)} %bitcast.6), channel_id=1, replica_groups=mesh['dp'=16,'row'=2,'col'=4] {'col'}, dimensions={0} | all-to-all | bytes 7864320 | tf_op jit(solution)/shard_map/all_to_all | solution.py:9
  79.6 20.9 %convolution_convert_fusion = bf16[2048,3584]{1,0:T(8,128)(2,1)} fusion(bf16[960,2048]{1,0:T(8,128)(2,1)S(1)} %bitcast.7, bf16[960,3584]{1,0:T(8,128)(2,1)} %bitcast.2), kind=kOutput, calls=%fused_computation | convolution fusion | flops 14100201472 | bytes 25493504 | tf_op jit(solution)/shard_map/dot_general | solution.py:29
  100.6 0.0 reduce-scatter.2.cloned.1.call-update
  100.6 103.1 %reduce-scatter.2.cloned.1.call-done = bf16[128,3584]{1,0:T(8,128)(2,1)} async-done(((bf16[2048,3584]{1,0:T(8,128)(2,1)}), bf16[128,3584]{1,0:T(8,128)(2,1)}) %reduce-scatter.2.cloned.1.call-update) | async-done | bytes 917520 | tf_op jit(solution)/shard_map/reduce_scatter | solution.py:42
Async XLA Ops:
  15.3 8.0 %copy-start = (bf16[240,2048]{1,0:T(8,128)(2,1)S(1)}, bf16[240,2048]{1,0:T(8,128)(2,1)}, u32[]{:S(2)}) copy-start(bf16[240,2048]{1,0:T(8,128)(2,1)} %param.4) | copy-start | bytes 2949124
  15.4 14.0 %all-to-all-start.1 = ((bf16[2,480,3584]{2,1,0:T(8,128)(2,1)}), bf16[2,480,3584]{2,1,0:T(8,128)(2,1)}, u32[]{:S(2)}, u32[]{:S(2)}) async-start(bf16[2,480,3584]{2,1,0:T(8,128)(2,1)} %broadcast_in_dim.3), calls=%async_computation.1 | async-start | bytes 13762560 | tf_op jit(solution)/shard_map/all_to_all | solution.py:14
  23.3 180.4 %reduce-scatter.2.cloned.1.call-start = ((), (), s32[]{:S(2)}) async-start(), calls=%async_computation.3 | async-start | bytes 15597568 | tf_op jit(solution)/shard_map/reduce_scatter | solution.py:42
Sparse Core Ops, SparseCore 0:
  100.7 102.9 reduce-scatter.1
